TPU v7x, 32 devices: a whole 2x2x4 slice. The times are simulated.
32 devices in a mesh: gx: 4 (over z), gy: 8 (over y, x, core).
Axes of the slice: x: 2, y: 2, z: 4, core: 2. Of those that a mesh axis runs over, the one named last changes fastest.
Arguments:
- splats: float32 [1024, 55, 128], P(('gx', 'gy')), as said below
- moment_one: float32 [1024, 55, 128], P(('gx', 'gy')), may hold values from -0.3 to 0.3
- moment_two: float32 [1024, 55, 128], P(('gx', 'gy')), may hold values from 0.001 to 1
- target: float32 [512, 3, 256], P(('gx', 'gy')), may hold values from 0 to 1
- tile_place: int32 [512], P(('gx', 'gy')), may hold values from 0 to 511, as said below
- pairs: int32 [512, 8], P(('gx', 'gy')), may hold values from -1 to 63, as said below
- fetch: int32 [32, 32, 2], P(('gx', 'gy')), may hold values from -1 to 31, as said below
Outputs:
- image: float32 [512, 3, 256], P(('gx', 'gy'))
- splat_grad: float32 [1024, 55, 128], P(('gx', 'gy'))
- adam_step: float32 [1024, 55, 128], P(('gx', 'gy'))
Inputs may be any that keep to these rules, and one draw needn't show every extreme that they name: fetch[d, o] lists up to 2 distinct blocks of owner o (indices among the owner's 32 blocks, owner o holding global blocks o * 32 to o * 32 + 31) that device d fetches; -1 marks an empty place; every device fetches 2 blocks from some owner. pairs[r] names distinct fetched places s = o * 2 + i of the device that holds row r, each with fetch[that device, o, i] >= 0; -1 marks empty places, which come last; on every device some row has all 8 places live. `tile_place`: a permutation of the view tiles; view tiles are numbered row by row, 16 to a row. z = splats[:, 2] lies between 2 and 12.
All inputs are finite; a program needn't handle non-finite values.
Results may differ from a plain program's by a relative error of at most 0.0003.
Values sent between devices are 32-bit elements; how exact they have to be, the bound alone decides.
A program may use at most 128 MiB of HBM per device.

v0:
```python
import functools

import jax
import jax.numpy as jnp
import numpy as np
from jax import lax
from jax.experimental import pallas as pl
from jax.experimental.pallas import tpu as pltpu
from jax.sharding import PartitionSpec as P

TX = 16
SIDE = 16
PIXELS = SIDE * SIDE
LOG2E = 1.4426950408889634
DEAD = -1.0e4
GROUP = 4
F32 = jnp.float32
BF16 = jnp.bfloat16


HARMONIC_ZERO = 0.28209479177387814
HARMONIC_ONE = 0.4886025119029199
HARMONIC_TWO = (
    1.0925484305920792,
    -1.0925484305920792,
    0.31539156525252005,
    -1.0925484305920792,
    0.5462742152960396,
)
HARMONIC_THREE = (
    -0.5900435899266435,
    2.890611442640554,
    -0.4570457994644658,
    0.3731763325901154,
    -0.4570457994644658,
    1.445305721320277,
    -0.5900435899266435,
)


def harmonics(east, north, ahead):
    east_east = east * east
    north_north = north * north
    ahead_ahead = ahead * ahead
    terms = [
        jnp.full_like(east, HARMONIC_ZERO),
        -HARMONIC_ONE * north,
        HARMONIC_ONE * ahead,
        -HARMONIC_ONE * east,
        HARMONIC_TWO[0] * east * north,
        HARMONIC_TWO[1] * north * ahead,
        HARMONIC_TWO[2] * (2.0 * ahead_ahead - east_east - north_north),
        HARMONIC_TWO[3] * east * ahead,
        HARMONIC_TWO[4] * (east_east - north_north),
        HARMONIC_THREE[0] * north * (3.0 * east_east - north_north),
        HARMONIC_THREE[1] * east * north * ahead,
        HARMONIC_THREE[2] * north * (4.0 * ahead_ahead - east_east - north_north),
        HARMONIC_THREE[3] * ahead * (2.0 * ahead_ahead - 3.0 * east_east - 3.0 * north_north),
        HARMONIC_THREE[4] * east * (4.0 * ahead_ahead - east_east - north_north),
        HARMONIC_THREE[5] * ahead * (east_east - north_north),
        HARMONIC_THREE[6] * east * (east_east - 3.0 * north_north),
    ]
    return jnp.stack(terms, axis=1)


def derive(raw, width, height):
    place_x = raw[:, 0]
    place_y = raw[:, 1]
    place_z = raw[:, 2]
    screen_u = width * place_x / place_z + 0.5 * width
    screen_v = width * place_y / place_z + 0.5 * height
    inverse_one = jnp.exp(-2.0 * raw[:, 3])
    inverse_two = jnp.exp(-2.0 * raw[:, 4])
    cosine = jnp.cos(raw[:, 5])
    sine = jnp.sin(raw[:, 5])
    conic_a = cosine * cosine * inverse_one + sine * sine * inverse_two
    conic_b = cosine * sine * (inverse_one - inverse_two)
    conic_c = sine * sine * inverse_one + cosine * cosine * inverse_two
    log_opacity = jax.nn.log_sigmoid(raw[:, 6])
    length = jnp.sqrt(place_x * place_x + place_y * place_y + place_z * place_z)
    basis = harmonics(place_x / length, place_y / length, place_z / length)
    coeffs = raw[:, 7:].reshape(raw.shape[0], 3, 16, raw.shape[2])
    colors = 0.5 + jnp.sum(coeffs * basis[:, None], axis=2)
    head = jnp.stack([screen_u, screen_v, conic_a, conic_b, conic_c, log_opacity], axis=1)
    return jnp.concatenate([head, colors], axis=1)


def pixel_basis():
    j = np.arange(PIXELS)
    x = j % SIDE + 0.5 - SIDE / 2
    y = j // SIDE + 0.5 - SIDE / 2
    rows = np.stack([x * x, x * y, y * y, x, y, np.ones_like(x), 0 * x, 0 * x])
    return np.concatenate([rows, rows, rows, 0 * rows]).astype(np.float32)


def lane_order(block):
    row = np.arange(block)
    splat = (row % 8) * (block // 8) + row // 8
    return (np.arange(block)[:, None] == splat[None, :]).astype(np.float32)


def rounded(x):
    return x.astype(BF16).astype(F32)


def shifted(x, shift):
    return pltpu.roll(x, shift % 8, 0)


def blend_kernel(
    pairs_ref, place_ref, basis_ref, arrived_ref, target_ref, image_ref, grad_ref,
    screen, coef, colour, alphas, weights, halves, products, steps, resid, moments, grads,
):
    step = pl.program_id(0)
    depth = pairs_ref.shape[1]
    block = arrived_ref.shape[2]
    chunks = block // 8
    sub = lax.broadcasted_iota(jnp.int32, (8, PIXELS), 0)
    sub_lane = lax.broadcasted_iota(jnp.int32, (8, block), 0)

    @pl.when(step == 0)
    def _():
        grad_ref[...] = jnp.zeros_like(grad_ref)
        coef[...] = jnp.zeros_like(coef)
        colour[...] = jnp.zeros_like(colour)
        resid[...] = jnp.zeros_like(resid)

    live = []
    centre = []
    deepest = jnp.int32(0)
    for t in range(GROUP):
        row = step * GROUP + t
        tile = place_ref[row]
        count = jnp.int32(0)
        for k in range(depth):
            slot = pairs_ref[row, k]
            count = count + (slot >= 0).astype(jnp.int32)
            screen[t, 0:9, k, :] = arrived_ref[jnp.maximum(slot, 0)]
        live.append(count)
        deepest = jnp.maximum(deepest, count)
        cx = (lax.rem(tile, TX) * SIDE + SIDE // 2).astype(F32)
        cy = (lax.div(tile, TX) * SIDE + SIDE // 2).astype(F32)
        centre.append((cx, cy))
        u = screen[t, 0] - cx
        v = screen[t, 1] - cy
        a, b, c = screen[t, 2], screen[t, 3], screen[t, 4]
        opac = jnp.maximum(screen[t, 5], DEAD)
        lin_x = a * u + b * v
        lin_y = b * u + c * v
        const = opac - 0.5 * (lin_x * u + lin_y * v)
        on = sub_lane < count
        for j, value in enumerate((-0.5 * a, -b, -0.5 * c, lin_x, lin_y, const)):
            coef[t, j] = jnp.where(on, LOG2E * value, DEAD if j == 5 else 0.0)
        for h in range(3):
            colour[t, h] = screen[t, 6 + h]

    basis = basis_ref[...].astype(BF16)
    zero8 = jnp.zeros((8, block), F32)
    zero_row = jnp.zeros((8, PIXELS), F32)

    def forward(k, carry):
        after = []
        for t in range(GROUP):
            trans, total = carry[2 * t], carry[2 * t + 1]
            c = coef[t, :, k, :]
            c1 = rounded(c)
            c2 = rounded(c - c1)
            c3 = c - c1 - c2
            parts = jnp.concatenate([c1, c2, c3, zero8], axis=0).astype(BF16)
            power = lax.dot_general(
                parts, basis, (((0,), (0,)), ((), ())), preferred_element_type=F32
            )
            alpha = jnp.exp2(power)
            alphas[t, k] = alpha
            keep = 1.0 - alpha
            kept = keep[0:8]
            for i in range(1, chunks):
                kept = kept * keep[8 * i : 8 * i + 8]
            products[t, k] = kept
            scan = jnp.where(sub == 0, trans, shifted(kept, 1))
            for d in (1, 2, 4):
                scan = scan * jnp.where(sub < d, 1.0, shifted(scan, d))
            trans = jnp.broadcast_to((scan * kept)[7:8], (8, PIXELS))
            here = scan
            for i in range(0, chunks, 2):
                one = alpha[8 * i : 8 * i + 8] * here
                here = here * keep[8 * i : 8 * i + 8]
                two = alpha[8 * i + 8 : 8 * i + 16] * here
                here = here * keep[8 * i + 8 : 8 * i + 16]
                pair = jnp.concatenate([one, two], axis=0)
                weights[t, k, 8 * i : 8 * i + 16] = pair
                high = pair.astype(BF16)
                halves[t, k, 8 * i : 8 * i + 16] = high
                halves[t, k, block + 8 * i : block + 8 * i + 16] = (
                    pair - high.astype(F32)
                ).astype(BF16)
            hue = colour[t, :, k, :]
            hue1 = rounded(hue)
            hue2 = hue - hue1
            left = jnp.concatenate(
                [
                    jnp.concatenate([hue1, hue1], axis=1),
                    jnp.concatenate([hue2, zero8], axis=1),
                ],
                axis=0,
            ).astype(BF16)
            total = total + jnp.dot(left, halves[t, k], preferred_element_type=F32)
            after += [trans, total]
        return tuple(after)

    start = (jnp.ones((8, PIXELS), F32), jnp.zeros((16, PIXELS), F32)) * GROUP
    done = lax.fori_loop(0, deepest, forward, start)

    slopes = []
    for t in range(GROUP):
        total = done[2 * t + 1]
        image = (total[0:8] + total[8:16])[0:3]
        image_ref[t] = image
        resid[t, 0:3] = (image - target_ref[t]) * (2.0 / 512.0)
        g = resid[t]
        g1 = rounded(g)
        g2 = g - g1
        slopes.append(
            (
                jnp.concatenate([g1, g1, g2, zero_row], axis=0).astype(BF16),
                jnp.concatenate([g1, g2], axis=0).astype(BF16),
            )
        )
    monomials = basis_ref[0:16].astype(BF16)

    def backward(index, carry):
        k = deepest - 1 - index
        after = []
        for t in range(GROUP):
            behind = carry[t]
            g3, g2 = slopes[t]
            hue = colour[t, :, k, :]
            hue1 = rounded(hue)
            hue2 = hue - hue1
            left = jnp.concatenate([hue1, hue2, hue1, zero8], axis=0).astype(BF16)
            slope = lax.dot_general(
                left, g3, (((0,), (0,)), ((), ())), preferred_element_type=F32
            )
            alpha = alphas[t, k]
            keep = 1.0 - alpha
            lit = alpha * slope
            gather = lit[block - 8 : block]
            for i in range(chunks - 2, -1, -1):
                gather = lit[8 * i : 8 * i + 8] + keep[8 * i : 8 * i + 8] * gather
            kept = products[t, k]
            scan = jnp.where(sub == 7, behind, shifted(gather, -1))
            rate = jnp.where(sub == 7, 0.0, shifted(kept, -1))
            for d in (1, 2, 4):
                inside = sub < 8 - d
                scan = scan + rate * jnp.where(inside, shifted(scan, -d), 0.0)
                rate = rate * jnp.where(inside, shifted(rate, -d), 1.0)
            after.append(jnp.broadcast_to((gather + kept * scan)[0:1], (8, PIXELS)))
            here = scan
            for i in range(chunks - 2, -1, -2):
                lo, mid, hi = 8 * i, 8 * i + 8, 8 * i + 16
                two = weights[t, k, mid:hi] * (slope[mid:hi] - here)
                here = lit[mid:hi] + keep[mid:hi] * here
                one = weights[t, k, lo:mid] * (slope[lo:mid] - here)
                here = lit[lo:mid] + keep[lo:mid] * here
                pair = jnp.concatenate([one, two], axis=0)
                high = pair.astype(BF16)
                steps[t, lo:hi] = high
                steps[t, block + lo : block + hi] = (pair - high.astype(F32)).astype(BF16)
            sums = lax.dot_general(
                monomials, steps[t], (((1,), (1,)), ((), ())), preferred_element_type=F32
            )
            moments[t, 0:8, k, :] = sums[0:8, 0:block] + sums[0:8, block:]
            hues = lax.dot_general(
                g2, halves[t, k], (((1,), (1,)), ((), ())), preferred_element_type=F32
            )
            moments[t, 8:16, k, :] = hues[0:8, 0:block] + hues[0:8, block:] + hues[8:16, 0:block]
        return tuple(after)

    lax.fori_loop(0, deepest, backward, (jnp.zeros((8, PIXELS), F32),) * GROUP)

    for t in range(GROUP):
        row = step * GROUP + t
        cx, cy = centre[t]
        u = screen[t, 0] - cx
        v = screen[t, 1] - cy
        a, b, c = screen[t, 2], screen[t, 3], screen[t, 4]
        mxx, mxy, myy = moments[t, 0], moments[t, 1], moments[t, 2]
        mx, my, m = moments[t, 3], moments[t, 4], moments[t, 5]
        off_x = mx - u * m
        off_y = my - v * m
        grads[t, 0] = a * off_x + b * off_y
        grads[t, 1] = b * off_x + c * off_y
        grads[t, 2] = -0.5 * (mxx - u * (mx + off_x))
        grads[t, 3] = -(mxy - u * my - v * off_x)
        grads[t, 4] = -0.5 * (myy - v * (my + off_y))
        grads[t, 5] = m
        for h in range(3):
            grads[t, 6 + h] = moments[t, 8 + h]
        for k in range(depth):

            @pl.when(k < live[t])
            def _():
                slot = pairs_ref[row, k]
                grad_ref[slot] = grad_ref[slot] + grads[t, 0:9, k, :]


def blend(arrived, target, tile_place, pairs):
    tiles, channels, pixels = target.shape
    depth = pairs.shape[1]
    slots, rows, block = arrived.shape
    basis = jnp.asarray(pixel_basis())
    whole = lambda s, *_: (0, 0, 0)
    return pl.pallas_call(
        blend_kernel,
        grid_spec=pltpu.PrefetchScalarGridSpec(
            num_scalar_prefetch=2,
            grid=(tiles // GROUP,),
            in_specs=[
                pl.BlockSpec(basis.shape, lambda s, *_: (0, 0)),
                pl.BlockSpec(arrived.shape, whole),
                pl.BlockSpec((GROUP, channels, pixels), lambda s, *_: (s, 0, 0)),
            ],
            out_specs=[
                pl.BlockSpec((GROUP, channels, pixels), lambda s, *_: (s, 0, 0)),
                pl.BlockSpec(arrived.shape, whole),
            ],
            scratch_shapes=[
                pltpu.VMEM((GROUP, 16, depth, block), F32),
                pltpu.VMEM((GROUP, 8, depth, block), F32),
                pltpu.VMEM((GROUP, 8, depth, block), F32),
                pltpu.VMEM((GROUP, depth, block, pixels), F32),
                pltpu.VMEM((GROUP, depth, block, pixels), F32),
                pltpu.VMEM((GROUP, depth, 2 * block, pixels), BF16),
                pltpu.VMEM((GROUP, depth, 8, pixels), F32),
                pltpu.VMEM((GROUP, 2 * block, pixels), BF16),
                pltpu.VMEM((GROUP, 8, pixels), F32),
                pltpu.VMEM((GROUP, 16, depth, block), F32),
                pltpu.VMEM((GROUP, 16, depth, block), F32),
            ],
        ),
        out_shape=[
            jax.ShapeDtypeStruct(target.shape, F32),
            jax.ShapeDtypeStruct(arrived.shape, F32),
        ],
        compiler_params=pltpu.CompilerParams(dimension_semantics=("arbitrary",)),
        name="blend",
    )(pairs, tile_place, basis, arrived, target)


def trade(payload):
    return lax.all_to_all(payload, ("gx", "gy"), split_axis=0, concat_axis=0, tiled=True)


def local(splats, moment_one, moment_two, target, tile_place, pairs, fetch):
    devices = lax.axis_size("gx") * lax.axis_size("gy")
    tiles_here = target.shape[0]
    width = 16.0 * TX
    height = 16.0 * (tiles_here * devices // TX)
    order = jnp.asarray(lane_order(splats.shape[2]))

    def project(raw):
        return jnp.dot(derive(raw, width, height), order, precision=lax.Precision.HIGHEST)

    asked = lax.all_to_all(fetch[0], ("gx", "gy"), split_axis=0, concat_axis=0, tiled=True)
    wanted = jnp.maximum(asked, 0)
    own_screen, own_pull = jax.vjp(project, splats)
    payload = own_screen[wanted]
    arrived = trade(payload)
    arrived = arrived.reshape((-1,) + payload.shape[2:])
    image, received_gradients = blend(arrived, target, tile_place, pairs)
    returned = trade(received_gradients.reshape(payload.shape))
    owner_pick = (asked.reshape(-1)[None, :] == jnp.arange(splats.shape[0])[:, None]).astype(
        jnp.float32
    )
    summed = jnp.dot(
        owner_pick, returned.reshape(owner_pick.shape[1], -1), precision=lax.Precision.HIGHEST
    )
    summed = summed.reshape((splats.shape[0],) + returned.shape[2:])
    (splat_grad,) = own_pull(summed)
    first = 0.9 * moment_one + 0.1 * splat_grad
    second_moment = 0.999 * moment_two + 0.001 * splat_grad * splat_grad
    adam_step = first / (jnp.sqrt(second_moment) + 1e-08)
    return (image, splat_grad, adam_step)


def solution(mesh):
    both = ("gx", "gy")
    return jax.shard_map(
        local,
        mesh=mesh,
        in_specs=(
            P(both, None, None),
            P(both, None, None),
            P(both, None, None),
            P(both, None, None),
            P(both),
            P(both, None),
            P(both, None, None),
        ),
        out_specs=(P(both, None, None), P(both, None, None), P(both, None, None)),
        check_vma=False,
    )
```

profile of v0, /device:TPU:0, one launch (start us, length us, event | category | flops | bytes accessed | tf_op | source)
XLA Modules:
  0.0 120.8 jit_solution(2006563123027152867)
XLA Ops:
  0.6 0.0 copy-start.7
  0.6 0.0 copy-start
  0.7 0.7 copy-done.7
  1.3 0.7 copy.24
  2.0 7.3 %all-to-all-start = ((s32[32,1,2]{2,1,0:T(1,128)}), s32[32,1,2]{2,1,0:T(1,128)S(1)}, u32[]{:S(2)}, u32[]{:S(2)}) async-start(s32[32,1,2]{2,1,0:T(1,128)} %copy.24), calls=%async_computation | async-start | bytes 32768 | tf_op jit(solution)/shard_map/all_to_all | solution.py:364
  9.3 1.2 slice.38
  10.5 0.0 copy-done
  10.6 0.1 constant_dynamic-update-slice_fusion.12
  10.7 0.1 constant_dynamic-update-slice_fusion.11
  10.8 0.1 constant_dynamic-update-slice_fusion.10
  11.0 0.1 multiply_reduce_fusion.1
  11.2 0.0 copy-start.3
  11.2 0.8 copy-done.3
  12.0 0.3 fusion.28
  12.3 0.1 copy.25
  12.4 4.1 %all-to-all-done = s32[32,1,2]{2,1,0:T(1,128)S(1)} async-done(((s32[32,1,2]{2,1,0:T(1,128)}), s32[32,1,2]{2,1,0:T(1,128)S(1)}, u32[]{:S(2)}, u32[]{:S(2)}) %all-to-all-start) | async-done | bytes 288 | tf_op jit(solution)/shard_map/all_to_all | solution.py:364
  16.4 0.5 broadcast.386
  16.9 0.7 fusion.27
  17.7 0.1 reshape.51
  17.8 0.6 gather_fusion
  18.4 0.9 copy.26
  19.3 0.0 copy-start.6
  19.3 0.0 copy-start.5
  19.3 2.7 %all-to-all-start.1 = ((f32[32,2,9,128]{3,1,2,0:T(2,128)}), f32[32,2,9,128]{3,1,2,0:T(2,128)S(1)}, u32[]{:S(2)}, u32[]{:S(2)}) async-start(f32[32,2,9,128]{3,1,2,0:T(2,128)} %copy.26), calls=%async_computation.1 | async-start | bytes 589824 | tf_op jit(solution)/shard_map/all_to_all | solution.py:351
  22.0 0.0 copy-done.6
  22.1 0.7 copy.28.pairs_ref
  22.7 0.0 copy-done.5
  22.7 0.7 copy.29.target_ref
  23.4 10.1 %all-to-all-done.1 = f32[32,2,9,128]{3,1,2,0:T(2,128)S(1)} async-done(((f32[32,2,9,128]{3,1,2,0:T(2,128)}), f32[32,2,9,128]{3,1,2,0:T(2,128)S(1)}, u32[]{:S(2)}, u32[]{:S(2)}) %all-to-all-start.1) | async-done | bytes 294944 | tf_op jit(solution)/shard_map/all_to_all | solution.py:351
  33.4 0.9 copy.27
  34.3 59.3 %blend.1 = (f32[16,3,256]{2,1,0:T(4,128)}, f32[64,9,128]{2,1,0:T(8,128)}) custom-call(s32[16,8]{1,0:T(8,128)} %copy.28.pairs_ref, s32[16]{0:T(128)} %place_ref.1, f32[32,256]{1,0:T(8,128)} %constant.71.clone.basis_ref, f32[64,9,128]{2,1,0:T(8,128)} %bitcast.31, f32[16,3,256]{2,1,0:T(4,128)} %copy.29.target_ref), custom_call_target="tpu_custom_call" | custom-call | tf_op jit(solution)/shard_map/blend/pallas_call | solution.py:313
  93.6 1.9 %copy.30 = f32[32,2,9,128]{3,1,2,0:T(2,128)} copy(f32[32,2,9,128]{3,2,1,0:T(8,128)} %bitcast.34) | data formatting | bytes 589824 | tf_op jit(solution)/shard_map/reshape | solution.py:371
  95.5 0.0 copy-start.4
  95.5 10.0 %all-to-all-start.2 = ((f32[32,2,9,128]{3,1,2,0:T(2,128)}), f32[32,2,9,128]{3,1,2,0:T(2,128)S(1)}, u32[]{:S(2)}, u32[]{:S(2)}) async-start(f32[32,2,9,128]{3,1,2,0:T(2,128)} %copy.30), calls=%async_computation.2 | async-start | bytes 589824 | tf_op jit(solution)/shard_map/all_to_all | solution.py:351
  105.5 0.1 eq.27
  105.6 0.0 copy-done.4
  105.6 0.6 copy.33
  106.2 10.7 %all-to-all-done.2 = f32[32,2,9,128]{3,1,2,0:T(2,128)S(1)} async-done(((f32[32,2,9,128]{3,1,2,0:T(2,128)}), f32[32,2,9,128]{3,1,2,0:T(2,128)S(1)}, u32[]{:S(2)}, u32[]{:S(2)}) %all-to-all-start.2) | async-done | bytes 294944 | tf_op jit(solution)/shard_map/all_to_all | solution.py:351
  116.9 0.1 copy.31
  116.9 0.3 fusion.4
  117.3 0.3 fusion.29
  117.6 0.1 fusion.7
  117.7 0.0 copy-start.1
  117.7 0.0 copy-start.2
  117.7 0.1 broadcast_multiply_fusion
  117.9 0.1 fusion.11
  118.0 0.1 fusion.17
  118.1 0.8 copy-done.1
  118.9 0.3 copy-done.2
  119.1 1.6 %fusion.3 = (f32[32,55,128]{2,0,1:T(8,128)}, f32[32,55,128]{2,0,1:T(8,128)}) fusion(f32[32,55,128]{2,0,1:T(8,128)S(1)} %copy-done.1, f32[32,55,128]{2,0,1:T(8,128)S(1)} %copy-done.2, f32[32,1,128]{2,0,1:T(8,128)S(1)} %get-tuple-element.35, f32[32,1,128]{2,0,1:T(8,128)S(1)} %get-tuple-element.36, f32[32,1,128]{2,0,1:T(8,128)S(1)} %get-tuple-element.20, ...), kind=kLoop, calls=%fused_computation.5 | loop fusion | flops 3829760 | bytes 4521984 | tf_op jit(solution)/shard_map/div | solution.py:382
  (16 shorter events, 0.2 us)
Async XLA Ops:
  0.6 0.7 copy-start.7
  0.6 9.9 %copy-start = (f32[32,55,128]{2,0,1:T(8,128)S(1)}, f32[32,55,128]{2,0,1:T(8,128)}, u32[]{:S(2)}) copy-start(f32[32,55,128]{2,0,1:T(8,128)} %param.9) | copy-start | bytes 2703364
  2.0 14.4 %all-to-all-start = ((s32[32,1,2]{2,1,0:T(1,128)}), s32[32,1,2]{2,1,0:T(1,128)S(1)}, u32[]{:S(2)}, u32[]{:S(2)}) async-start(s32[32,1,2]{2,1,0:T(1,128)} %copy.24), calls=%async_computation | async-start | bytes 32768 | tf_op jit(solution)/shard_map/all_to_all | solution.py:364
  11.2 0.8 copy-start.3
  19.3 2.7 %copy-start.6 = (s32[16,8]{0,1:T(8,128)S(1)}, s32[16,8]{0,1:T(8,128)}, u32[]{:S(2)}) copy-start(s32[16,8]{0,1:T(8,128)} %param.14) | copy-start | bytes 1540
  19.3 3.4 %copy-start.5 = (f32[16,3,256]{2,0,1:T(8,128)S(1)}, f32[16,3,256]{2,0,1:T(8,128)}, u32[]{:S(2)}) copy-start(f32[16,3,256]{2,0,1:T(8,128)} %param.12) | copy-start | bytes 147460
  19.3 14.1 %all-to-all-start.1 = ((f32[32,2,9,128]{3,1,2,0:T(2,128)}), f32[32,2,9,128]{3,1,2,0:T(2,128)S(1)}, u32[]{:S(2)}, u32[]{:S(2)}) async-start(f32[32,2,9,128]{3,1,2,0:T(2,128)} %copy.26), calls=%async_computation.1 | async-start | bytes 589824 | tf_op jit(solution)/shard_map/all_to_all | solution.py:351
  95.5 10.1 %copy-start.4 = (f32[16,3,256]{2,1,0:T(4,128)S(1)}, f32[16,3,256]{2,1,0:T(4,128)}, u32[]{:S(2)}) copy-start(f32[16,3,256]{2,1,0:T(4,128)} %get-tuple-element.13) | copy-start | bytes 147460
  95.5 21.4 %all-to-all-start.2 = ((f32[32,2,9,128]{3,1,2,0:T(2,128)}), f32[32,2,9,128]{3,1,2,0:T(2,128)S(1)}, u32[]{:S(2)}, u32[]{:S(2)}) async-start(f32[32,2,9,128]{3,1,2,0:T(2,128)} %copy.30), calls=%async_computation.2 | async-start | bytes 589824 | tf_op jit(solution)/shard_map/all_to_all | solution.py:351
  117.7 1.2 copy-start.1
  117.7 1.4 %copy-start.2 = (f32[32,55,128]{2,0,1:T(8,128)S(1)}, f32[32,55,128]{2,0,1:T(8,128)}, u32[]{:S(2)}) copy-start(f32[32,55,128]{2,0,1:T(8,128)} %param.10) | copy-start | bytes 2703364
where the time goes:
time: 122 us; the launch traced here: 121 us
  Pallas kernels  59.3 us (49%)
  waiting for transfers between devices  24.8 us (20%)
  starting transfers between devices  20 us (16%)
  local copies, waits for them, and re-layouts  11.5 us (9%)
  other arithmetic  3.34 us (3%)
    pallas_call x1, Pallas kernels, blend(): pl.pallas_call(blend_kernel, grid_spec=pltpu.PrefetchScalarGridSpec(num_s...  59.3 us
    all_to_all x2, waiting for transfers between devices, trade(): lax.all_to_all(payload, ('gx', 'gy'), split_axis=0, concat_axis=0, tiled=...  20.7 us
    all_to_all x2, starting transfers between devices, trade(): lax.all_to_all(payload, ('gx', 'gy'), split_axis=0, concat_axis=0, tiled=...  12.7 us
    all_to_all x1, starting transfers between devices, local(): lax.all_to_all(fetch[0], ('gx', 'gy'), split_axis=0, concat_axis=0, tiled...  7.33 us
    unnamed x20, local copies, waits for them, and re-layouts  4.53 us
    all_to_all x1, waiting for transfers between devices, local(): lax.all_to_all(fetch[0], ('gx', 'gy'), split_axis=0, concat_axis=0, tiled...  4.06 us
  transfers between devices with their start and end apart: 3, of which 3 were waited for; matrix products, arithmetic and copies ran while one was open for 3% of the time, Pallas kernels for 0%

commit v1 on v0

v1 whole, which is shorter than its diff:
```python
import functools

import jax
import jax.numpy as jnp
import numpy as np
from jax import lax
from jax.experimental import pallas as pl
from jax.experimental.pallas import tpu as pltpu
from jax.sharding import PartitionSpec as P

TX = 16
SIDE = 16
PIXELS = SIDE * SIDE
LOG2E = 1.4426950408889634
DEAD = -1.0e4
GROUP = 4
F32 = jnp.float32
BF16 = jnp.bfloat16


HARMONIC_ZERO = 0.28209479177387814
HARMONIC_ONE = 0.4886025119029199
HARMONIC_TWO = (
    1.0925484305920792,
    -1.0925484305920792,
    0.31539156525252005,
    -1.0925484305920792,
    0.5462742152960396,
)
HARMONIC_THREE = (
    -0.5900435899266435,
    2.890611442640554,
    -0.4570457994644658,
    0.3731763325901154,
    -0.4570457994644658,
    1.445305721320277,
    -0.5900435899266435,
)


def harmonics(east, north, ahead):
    east_east = east * east
    north_north = north * north
    ahead_ahead = ahead * ahead
    terms = [
        jnp.full_like(east, HARMONIC_ZERO),
        -HARMONIC_ONE * north,
        HARMONIC_ONE * ahead,
        -HARMONIC_ONE * east,
        HARMONIC_TWO[0] * east * north,
        HARMONIC_TWO[1] * north * ahead,
        HARMONIC_TWO[2] * (2.0 * ahead_ahead - east_east - north_north),
        HARMONIC_TWO[3] * east * ahead,
        HARMONIC_TWO[4] * (east_east - north_north),
        HARMONIC_THREE[0] * north * (3.0 * east_east - north_north),
        HARMONIC_THREE[1] * east * north * ahead,
        HARMONIC_THREE[2] * north * (4.0 * ahead_ahead - east_east - north_north),
        HARMONIC_THREE[3] * ahead * (2.0 * ahead_ahead - 3.0 * east_east - 3.0 * north_north),
        HARMONIC_THREE[4] * east * (4.0 * ahead_ahead - east_east - north_north),
        HARMONIC_THREE[5] * ahead * (east_east - north_north),
        HARMONIC_THREE[6] * east * (east_east - 3.0 * north_north),
    ]
    return jnp.stack(terms, axis=1)


def derive(raw, width, height):
    place_x = raw[:, 0]
    place_y = raw[:, 1]
    place_z = raw[:, 2]
    screen_u = width * place_x / place_z + 0.5 * width
    screen_v = width * place_y / place_z + 0.5 * height
    inverse_one = jnp.exp(-2.0 * raw[:, 3])
    inverse_two = jnp.exp(-2.0 * raw[:, 4])
    cosine = jnp.cos(raw[:, 5])
    sine = jnp.sin(raw[:, 5])
    conic_a = cosine * cosine * inverse_one + sine * sine * inverse_two
    conic_b = cosine * sine * (inverse_one - inverse_two)
    conic_c = sine * sine * inverse_one + cosine * cosine * inverse_two
    log_opacity = jax.nn.log_sigmoid(raw[:, 6])
    length = jnp.sqrt(place_x * place_x + place_y * place_y + place_z * place_z)
    basis = harmonics(place_x / length, place_y / length, place_z / length)
    coeffs = raw[:, 7:].reshape(raw.shape[0], 3, 16, raw.shape[2])
    colors = 0.5 + jnp.sum(coeffs * basis[:, None], axis=2)
    head = jnp.stack([screen_u, screen_v, conic_a, conic_b, conic_c, log_opacity], axis=1)
    return jnp.concatenate([head, colors], axis=1)


def pixel_basis():
    j = np.arange(PIXELS)
    x = j % SIDE + 0.5 - SIDE / 2
    y = j // SIDE + 0.5 - SIDE / 2
    rows = np.stack([x * x, x * y, y * y, x, y, np.ones_like(x), 0 * x, 0 * x])
    return np.concatenate([rows, rows, rows, 0 * rows]).astype(np.float32)


def lane_order(block):
    row = np.arange(block)
    splat = (row % 8) * (block // 8) + row // 8
    return (np.arange(block)[:, None] == splat[None, :]).astype(np.float32)


def rounded(x):
    return x.astype(BF16).astype(F32)


def shifted(x, shift):
    return pltpu.roll(x, shift % 8, 0)


def blend_kernel(
    pairs_ref, place_ref, order_ref, basis_ref, arrived_ref, target_ref, image_ref, grad_ref,
    screen, parts, hue_sum, hue_back, alphas, keeps, weights, halves, ends, slopes, steps, resid, moments,
):
    tiles, depth = pairs_ref.shape
    slots, rows, block = arrived_ref.shape
    chunks = block // 8
    sub = lax.broadcasted_iota(jnp.int32, (8, PIXELS), 0)

    grad_ref[...] = jnp.zeros_like(grad_ref)
    resid[...] = jnp.zeros_like(resid)
    parts[...] = jnp.zeros_like(parts)
    hue_sum[...] = jnp.zeros_like(hue_sum)
    hue_back[...] = jnp.zeros_like(hue_back)

    def prepare(s, _):
        screen[s, 0:rows] = arrived_ref[s]
        hue = jnp.concatenate([arrived_ref[s, 6:9], jnp.zeros((5, block), F32)], axis=0)
        hue1 = rounded(hue)
        hue2 = hue - hue1
        zero = jnp.zeros_like(hue)
        hue_sum[s] = jnp.concatenate(
            [
                jnp.concatenate([hue1, hue1], axis=1),
                jnp.concatenate([hue2, zero], axis=1),
            ],
            axis=0,
        ).astype(BF16)
        hue_back[s] = jnp.concatenate([hue1, hue2, hue1, zero], axis=0).astype(BF16)
        return 0

    lax.fori_loop(0, slots, prepare, 0)
    screen[slots] = jnp.zeros((16, block), F32)
    screen[slots, 5:6] = jnp.full((1, block), DEAD, F32)

    basis = basis_ref[...].astype(BF16)
    monomials = basis_ref[0:8].astype(BF16)
    zero_row = jnp.zeros((8, PIXELS), F32)

    def group(step, _):
        row = [order_ref[step * GROUP + t] for t in range(GROUP)]
        deepest = jnp.int32(0)
        centre = []
        for t in range(GROUP):
            tile = place_ref[row[t]]
            count = jnp.int32(0)
            for k in range(depth):
                count = count + (pairs_ref[row[t], k] >= 0).astype(jnp.int32)
            deepest = jnp.maximum(deepest, count)
            cx = (lax.rem(tile, TX) * SIDE + SIDE // 2).astype(F32)
            cy = (lax.div(tile, TX) * SIDE + SIDE // 2).astype(F32)
            centre.append((cx, cy))

        def place(t, k):
            slot = pairs_ref[row[t], k]
            return jnp.where(slot >= 0, slot, slots)

        def shape_up(k, _):
            for t in range(GROUP):
                cx, cy = centre[t]
                s = place(t, k)
                u = screen[s, 0:1] - cx
                v = screen[s, 1:2] - cy
                a, b, c = screen[s, 2:3], screen[s, 3:4], screen[s, 4:5]
                opac = jnp.maximum(screen[s, 5:6], DEAD)
                lin_x = a * u + b * v
                lin_y = b * u + c * v
                const = opac - 0.5 * (lin_x * u + lin_y * v)
                for j, value in enumerate((-0.5 * a, -b, -0.5 * c, lin_x, lin_y, const)):
                    parts[t, k, j : j + 1] = LOG2E * value
            return 0

        lax.fori_loop(0, deepest, shape_up, 0)

        def forward(k, carry):
            after = []
            for t in range(GROUP):
                trans, total = carry[2 * t], carry[2 * t + 1]
                c = parts[t, k]
                c1 = rounded(c)
                c2 = rounded(c - c1)
                c3 = c - c1 - c2
                left = jnp.concatenate([c1, c2, c3, jnp.zeros_like(c)], axis=0).astype(BF16)
                power = lax.dot_general(
                    left, basis, (((0,), (0,)), ((), ())), preferred_element_type=F32
                )
                alpha = jnp.exp2(power)
                keep = 1.0 - alpha
                alphas[t] = alpha
                keeps[t, k] = keep
                kept = keep[0:8]
                for i in range(1, chunks):
                    kept = kept * keep[8 * i : 8 * i + 8]
                scan = jnp.where(sub == 0, trans, shifted(kept, 1))
                for d in (1, 2, 4):
                    scan = scan * jnp.where(sub < d, 1.0, shifted(scan, d))
                end = scan * kept
                ends[t, k] = end
                trans = jnp.broadcast_to(end[7:8], (8, PIXELS))
                here = scan
                for i in range(0, chunks, 2):
                    lo, mid, hi = 8 * i, 8 * i + 8, 8 * i + 16
                    one = alphas[t, lo:mid] * here
                    here = here * keeps[t, k, lo:mid]
                    two = alphas[t, mid:hi] * here
                    here = here * keeps[t, k, mid:hi]
                    pair = jnp.concatenate([one, two], axis=0)
                    weights[t, k, lo:hi] = pair
                    high = pair.astype(BF16)
                    halves[t, k, lo:hi] = high
                    halves[t, k, block + lo : block + hi] = (pair - high.astype(F32)).astype(BF16)
                total = total + jnp.dot(
                    hue_sum[place(t, k)], halves[t, k], preferred_element_type=F32
                )
                after += [trans, total]
            return tuple(after)

        start = (jnp.ones((8, PIXELS), F32), jnp.zeros((16, PIXELS), F32)) * GROUP
        done = lax.fori_loop(0, deepest, forward, start)

        pulls = []
        for t in range(GROUP):
            total = done[2 * t + 1]
            image = (total[0:8] + total[8:16])[0:3]
            image_ref[row[t]] = image
            resid[t, 0:3] = (image - target_ref[row[t]]) * (2.0 / 512.0)
            g = resid[t]
            g1 = rounded(g)
            g2 = g - g1
            pulls.append(
                (
                    jnp.concatenate([g1, g1, g2, zero_row], axis=0).astype(BF16),
                    jnp.concatenate([g1, g2], axis=0).astype(BF16),
                )
            )

        def backward(index, carry):
            k = deepest - 1 - index
            after = []
            for t in range(GROUP):
                behind = carry[t]
                g3, g2 = pulls[t]
                slope = lax.dot_general(
                    hue_back[place(t, k)], g3, (((0,), (0,)), ((), ())), preferred_element_type=F32
                )
                slopes[t] = slope
                lit = weights[t, k] * slope
                run = lit[0:8]
                for i in range(1, chunks):
                    run = run + lit[8 * i : 8 * i + 8]
                scan = jnp.where(sub == 7, behind, shifted(run, -1))
                for d in (1, 2, 4):
                    scan = scan + jnp.where(sub < 8 - d, shifted(scan, -d), 0.0)
                after.append(jnp.broadcast_to((run + scan)[0:1], (8, PIXELS)))
                here = scan / jnp.maximum(ends[t, k], 1e-37)
                for i in range(chunks - 2, -1, -2):
                    lo, mid, hi = 8 * i, 8 * i + 8, 8 * i + 16
                    ahead = slopes[t, mid:hi]
                    gap = ahead - here
                    two = weights[t, k, mid:hi] * gap
                    here = ahead - keeps[t, k, mid:hi] * gap
                    ahead = slopes[t, lo:mid]
                    gap = ahead - here
                    one = weights[t, k, lo:mid] * gap
                    here = ahead - keeps[t, k, lo:mid] * gap
                    pair = jnp.concatenate([one, two], axis=0)
                    high = pair.astype(BF16)
                    steps[t, lo:hi] = high
                    steps[t, block + lo : block + hi] = (pair - high.astype(F32)).astype(BF16)
                sums = lax.dot_general(
                    monomials, steps[t], (((1,), (1,)), ((), ())), preferred_element_type=F32
                )
                moments[t, k, 0:8] = sums[:, 0:block] + sums[:, block:]
                hues = lax.dot_general(
                    g2, halves[t, k], (((1,), (1,)), ((), ())), preferred_element_type=F32
                )
                moments[t, k, 8:16] = (
                    hues[0:8, 0:block] + hues[0:8, block:] + hues[8:16, 0:block]
                )
            return tuple(after)

        lax.fori_loop(0, deepest, backward, (jnp.zeros((8, PIXELS), F32),) * GROUP)

        def settle(k, _):
            for t in range(GROUP):
                cx, cy = centre[t]
                s = place(t, k)
                u = screen[s, 0:1] - cx
                v = screen[s, 1:2] - cy
                a, b, c = screen[s, 2:3], screen[s, 3:4], screen[s, 4:5]
                mxx, mxy, myy = (moments[t, k, j : j + 1] for j in (0, 1, 2))
                mx, my, m = (moments[t, k, j : j + 1] for j in (3, 4, 5))
                off_x = mx - u * m
                off_y = my - v * m
                changes = (
                    a * off_x + b * off_y,
                    b * off_x + c * off_y,
                    -0.5 * (mxx - u * (mx + off_x)),
                    -(mxy - u * my - v * off_x),
                    -0.5 * (myy - v * (my + off_y)),
                    m,
                    moments[t, k, 8:9],
                    moments[t, k, 9:10],
                    moments[t, k, 10:11],
                )
                for j, change in enumerate(changes):
                    grad_ref[s, j : j + 1] = grad_ref[s, j : j + 1] + change
            return 0

        lax.fori_loop(0, deepest, settle, 0)
        return 0

    lax.fori_loop(0, tiles // GROUP, group, 0)


def deepest_first(pairs):
    live = jnp.sum((pairs >= 0).astype(jnp.int32), axis=1)
    row = jnp.arange(pairs.shape[0], dtype=jnp.int32)
    before = (live[None, :] > live[:, None]) | (
        (live[None, :] == live[:, None]) & (row[None, :] < row[:, None])
    )
    rank = jnp.sum(before.astype(jnp.int32), axis=1)
    return jnp.sum(jnp.where(rank[None, :] == row[:, None], row[None, :], 0), axis=1)


def blend(arrived, target, tile_place, pairs):
    tiles, channels, pixels = target.shape
    depth = pairs.shape[1]
    slots, rows, block = arrived.shape
    basis = jnp.asarray(pixel_basis())
    smem = pl.BlockSpec(memory_space=pltpu.SMEM)
    vmem = pl.BlockSpec(memory_space=pltpu.VMEM)
    image, grads = pl.pallas_call(
        blend_kernel,
        in_specs=[smem, smem, smem, vmem, vmem, vmem],
        out_specs=[vmem, vmem],
        scratch_shapes=[
            pltpu.VMEM((slots + 1, 16, block), F32),
            pltpu.VMEM((GROUP, depth, 8, block), F32),
            pltpu.VMEM((slots + 1, 16, 2 * block), BF16),
            pltpu.VMEM((slots + 1, 32, block), BF16),
            pltpu.VMEM((GROUP, block, pixels), F32),
            pltpu.VMEM((GROUP, depth, block, pixels), F32),
            pltpu.VMEM((GROUP, depth, block, pixels), F32),
            pltpu.VMEM((GROUP, depth, 2 * block, pixels), BF16),
            pltpu.VMEM((GROUP, depth, 8, pixels), F32),
            pltpu.VMEM((GROUP, block, pixels), F32),
            pltpu.VMEM((GROUP, 2 * block, pixels), BF16),
            pltpu.VMEM((GROUP, 8, pixels), F32),
            pltpu.VMEM((GROUP, depth, 16, block), F32),
        ],
        out_shape=[
            jax.ShapeDtypeStruct(target.shape, F32),
            jax.ShapeDtypeStruct((slots + 1, rows, block), F32),
        ],
        name="blend",
    )(pairs, tile_place, deepest_first(pairs), basis, arrived, target)
    return image, grads[:slots]


def trade(payload):
    return lax.all_to_all(payload, ("gx", "gy"), split_axis=0, concat_axis=0, tiled=True)


def local(splats, moment_one, moment_two, target, tile_place, pairs, fetch):
    devices = lax.axis_size("gx") * lax.axis_size("gy")
    tiles_here = target.shape[0]
    width = 16.0 * TX
    height = 16.0 * (tiles_here * devices // TX)
    order = jnp.asarray(lane_order(splats.shape[2]))

    def project(raw):
        return jnp.dot(derive(raw, width, height), order, precision=lax.Precision.HIGHEST)

    asked = lax.all_to_all(fetch[0], ("gx", "gy"), split_axis=0, concat_axis=0, tiled=True)
    wanted = jnp.maximum(asked, 0)
    own_screen, own_pull = jax.vjp(project, splats)
    payload = own_screen[wanted]
    arrived = trade(payload)
    arrived = arrived.reshape((-1,) + payload.shape[2:])
    image, received_gradients = blend(arrived, target, tile_place, pairs)
    returned = trade(received_gradients.reshape(payload.shape))
    owner_pick = (asked.reshape(-1)[None, :] == jnp.arange(splats.shape[0])[:, None]).astype(
        jnp.float32
    )
    summed = jnp.dot(
        owner_pick, returned.reshape(owner_pick.shape[1], -1), precision=lax.Precision.HIGHEST
    )
    summed = summed.reshape((splats.shape[0],) + returned.shape[2:])
    (splat_grad,) = own_pull(summed)
    first = 0.9 * moment_one + 0.1 * splat_grad
    second_moment = 0.999 * moment_two + 0.001 * splat_grad * splat_grad
    adam_step = first / (jnp.sqrt(second_moment) + 1e-08)
    return (image, splat_grad, adam_step)


def solution(mesh):
    both = ("gx", "gy")
    return jax.shard_map(
        local,
        mesh=mesh,
        in_specs=(
            P(both, None, None),
            P(both, None, None),
            P(both, None, None),
            P(both, None, None),
            P(both),
            P(both, None),
            P(both, None, None),
        ),
        out_specs=(P(both, None, None), P(both, None, None), P(both, None, None)),
        check_vma=False,
    )
```

time: 122 us -> 108 us (0.89)
  Pallas kernels: 59.3 us -> 44.9 us
    pallas_call x1, Pallas kernels: 59.3 us -> 44.9 us  [blend(): pl.pallas_call(blend_kernel, in_specs=[smem, smem, smem, vmem, vmem, vmem...]
  transfers between devices with their start and end apart: 3 -> 3, of which waited for: 3 -> 3; matrix products, arithmetic and copies ran while one was open for 3% -> 5% of each run, Pallas kernels for 0% -> 0%
where the time goes in v1:
time: 108 us; the launch traced here: 107 us
  Pallas kernels  44.9 us (42%)
  waiting for transfers between devices  23.9 us (22%)
  starting transfers between devices  21 us (19%)
  local copies, waits for them, and re-layouts  11.6 us (11%)
  other arithmetic  4.21 us (4%)
    pallas_call x1, Pallas kernels, blend(): pl.pallas_call(blend_kernel, in_specs=[smem, smem, smem, vmem, vmem, vmem...  44.9 us
    all_to_all x2, waiting for transfers between devices, trade(): lax.all_to_all(payload, ('gx', 'gy'), split_axis=0, concat_axis=0, tiled=...  19.8 us
    all_to_all x2, starting transfers between devices, trade(): lax.all_to_all(payload, ('gx', 'gy'), split_axis=0, concat_axis=0, tiled=...  13.7 us
    all_to_all x1, starting transfers between devices, local(): lax.all_to_all(fetch[0], ('gx', 'gy'), split_axis=0, concat_axis=0, tiled...  7.33 us
    unnamed x20, local copies, waits for them, and re-layouts  4.54 us
    all_to_all x1, waiting for transfers between devices, local(): lax.all_to_all(fetch[0], ('gx', 'gy'), split_axis=0, concat_axis=0, tiled...  4.06 us
  transfers between devices with their start and end apart: 3, of which 3 were waited for; matrix products, arithmetic and copies ran while one was open for 5% of the time, Pallas kernels for 0%

profile of v1, /device:TPU:0, one launch (start us, length us, event | category | flops | bytes accessed | tf_op | source)
XLA Modules:
  0.0 107.4 jit_solution(16416294335563865337)
XLA Ops:
  0.6 0.0 copy-start.7
  0.6 0.0 copy-start
  0.7 0.7 copy-done.7
  1.3 0.7 copy.34
  2.0 7.3 %all-to-all-start = ((s32[32,1,2]{2,1,0:T(1,128)}), s32[32,1,2]{2,1,0:T(1,128)S(1)}, u32[]{:S(2)}, u32[]{:S(2)}) async-start(s32[32,1,2]{2,1,0:T(1,128)} %copy.34), calls=%async_computation | async-start | bytes 32768 | tf_op jit(solution)/shard_map/all_to_all | solution.py:384
  9.3 1.2 %slice.41 = f32[32,48,128]{2,0,1:T(8,128)S(1)} slice(f32[32,55,128]{2,0,1:T(8,128)} %param.9), slice={[0:32], [7:55], [0:128]} | slice | bytes 1572864 | tf_op jit(solution)/shard_map/jvp()/slice | solution.py:82
  10.5 0.0 copy-done
  10.6 0.1 constant_dynamic-update-slice_fusion.12
  10.7 0.1 constant_dynamic-update-slice_fusion.11
  10.8 0.1 constant_dynamic-update-slice_fusion.10
  11.0 0.1 multiply_reduce_fusion.1
  11.2 0.0 copy-start.3
  11.2 0.8 copy-done.3
  12.0 0.3 fusion.30
  12.3 0.1 copy.35
  12.4 4.1 %all-to-all-done = s32[32,1,2]{2,1,0:T(1,128)S(1)} async-done(((s32[32,1,2]{2,1,0:T(1,128)}), s32[32,1,2]{2,1,0:T(1,128)S(1)}, u32[]{:S(2)}, u32[]{:S(2)}) %all-to-all-start) | async-done | bytes 288 | tf_op jit(solution)/shard_map/all_to_all | solution.py:384
  16.4 0.5 broadcast.389
  16.9 0.7 fusion.29
  17.7 0.1 reshape.54
  17.8 0.6 gather_fusion
  18.4 0.9 copy.36
  19.3 0.0 copy-start.6
  19.3 0.0 copy-start.5
  19.3 2.7 %all-to-all-start.1 = ((f32[32,2,9,128]{3,1,2,0:T(2,128)}), f32[32,2,9,128]{3,1,2,0:T(2,128)S(1)}, u32[]{:S(2)}, u32[]{:S(2)}) async-start(f32[32,2,9,128]{3,1,2,0:T(2,128)} %copy.36), calls=%async_computation.1 | async-start | bytes 589824 | tf_op jit(solution)/shard_map/all_to_all | solution.py:371
  22.0 0.0 copy-done.6
  22.1 0.7 copy.38.pairs_ref
  22.7 0.0 copy-done.5
  22.7 0.7 copy.39.target_ref
  23.4 0.2 convert_reduce_fusion
  23.6 0.7 select_reduce_fusion.order_ref
  24.3 9.2 %all-to-all-done.1 = f32[32,2,9,128]{3,1,2,0:T(2,128)S(1)} async-done(((f32[32,2,9,128]{3,1,2,0:T(2,128)}), f32[32,2,9,128]{3,1,2,0:T(2,128)S(1)}, u32[]{:S(2)}, u32[]{:S(2)}) %all-to-all-start.1) | async-done | bytes 294944 | tf_op jit(solution)/shard_map/all_to_all | solution.py:371
  33.4 0.9 copy.37
  34.3 44.9 %blend.1 = (f32[16,3,256]{2,1,0:T(4,128)}, f32[65,9,128]{2,1,0:T(8,128)}) custom-call(s32[16,8]{1,0:T(8,128)} %copy.38.pairs_ref, s32[16]{0:T(128)} %place_ref.1, s32[16]{0:T(128)} %select_reduce_fusion.order_ref, f32[32,256]{1,0:T(8,128)} %constant.73.clone.basis_ref, f32[64,9,128]{2,1,0:T(8,128)} %bitcast.31, f32[16,3,256]{2,1,0:T(4,128)} %copy.39.target_ref), custom_call_target="tpu_custom_call" | custom-call | tf_op jit(solution)/shard_map/blend/pallas_call | solution.py:342
  79.2 1.1 %slice.42 = f32[64,9,128]{2,1,0:T(8,128)S(1)} slice(f32[65,9,128]{2,1,0:T(8,128)} %get-tuple-element.6), slice={[0:64], [0:9], [0:128]} | slice | bytes 589824 | tf_op jit(solution)/shard_map/slice | solution.py:367
  80.3 0.9 copy.40
  81.1 0.0 copy-start.4
  81.1 10.9 %all-to-all-start.2 = ((f32[32,2,9,128]{3,1,2,0:T(2,128)}), f32[32,2,9,128]{3,1,2,0:T(2,128)S(1)}, u32[]{:S(2)}, u32[]{:S(2)}) async-start(f32[32,2,9,128]{3,1,2,0:T(2,128)} %copy.40), calls=%async_computation.2 | async-start | bytes 589824 | tf_op jit(solution)/shard_map/all_to_all | solution.py:371
  92.1 0.1 eq.50
  92.2 0.0 copy-done.4
  92.2 0.6 copy.43
  92.8 10.7 %all-to-all-done.2 = f32[32,2,9,128]{3,1,2,0:T(2,128)S(1)} async-done(((f32[32,2,9,128]{3,1,2,0:T(2,128)}), f32[32,2,9,128]{3,1,2,0:T(2,128)S(1)}, u32[]{:S(2)}, u32[]{:S(2)}) %all-to-all-start.2) | async-done | bytes 294944 | tf_op jit(solution)/shard_map/all_to_all | solution.py:371
  103.5 0.1 copy.41
  103.5 0.3 fusion.4
  103.9 0.3 fusion.31
  104.2 0.1 fusion.7
  104.3 0.0 copy-start.1
  104.3 0.0 copy-start.2
  104.3 0.1 broadcast_multiply_fusion
  104.4 0.1 fusion.11
  104.6 0.1 fusion.17
  104.7 0.8 copy-done.1
  105.5 0.3 copy-done.2
  105.7 1.6 %fusion.3 = (f32[32,55,128]{2,0,1:T(8,128)}, f32[32,55,128]{2,0,1:T(8,128)}) fusion(f32[32,55,128]{2,0,1:T(8,128)S(1)} %copy-done.1, f32[32,55,128]{2,0,1:T(8,128)S(1)} %copy-done.2, f32[32,1,128]{2,0,1:T(8,128)S(1)} %get-tuple-element.38, f32[32,1,128]{2,0,1:T(8,128)S(1)} %get-tuple-element.39, f32[32,1,128]{2,0,1:T(8,128)S(1)} %get-tuple-element.23, ...), kind=kLoop, calls=%fused_computation.5 | loop fusion | flops 3829760 | bytes 4521984 | tf_op jit(solution)/shard_map/div | solution.py:402
  (17 shorter events, 0.2 us)
Async XLA Ops:
  0.6 0.7 copy-start.7
  0.6 9.9 %copy-start = (f32[32,55,128]{2,0,1:T(8,128)S(1)}, f32[32,55,128]{2,0,1:T(8,128)}, u32[]{:S(2)}) copy-start(f32[32,55,128]{2,0,1:T(8,128)} %param.9) | copy-start | bytes 2703364
  2.0 14.4 %all-to-all-start = ((s32[32,1,2]{2,1,0:T(1,128)}), s32[32,1,2]{2,1,0:T(1,128)S(1)}, u32[]{:S(2)}, u32[]{:S(2)}) async-start(s32[32,1,2]{2,1,0:T(1,128)} %copy.34), calls=%async_computation | async-start | bytes 32768 | tf_op jit(solution)/shard_map/all_to_all | solution.py:384
  11.2 0.8 copy-start.3
  19.3 2.7 %copy-start.6 = (s32[16,8]{0,1:T(8,128)S(1)}, s32[16,8]{0,1:T(8,128)}, u32[]{:S(2)}) copy-start(s32[16,8]{0,1:T(8,128)} %param.14) | copy-start | bytes 1540
  19.3 3.4 %copy-start.5 = (f32[16,3,256]{2,0,1:T(8,128)S(1)}, f32[16,3,256]{2,0,1:T(8,128)}, u32[]{:S(2)}) copy-start(f32[16,3,256]{2,0,1:T(8,128)} %param.12) | copy-start | bytes 147460
  19.3 14.1 %all-to-all-start.1 = ((f32[32,2,9,128]{3,1,2,0:T(2,128)}), f32[32,2,9,128]{3,1,2,0:T(2,128)S(1)}, u32[]{:S(2)}, u32[]{:S(2)}) async-start(f32[32,2,9,128]{3,1,2,0:T(2,128)} %copy.36), calls=%async_computation.1 | async-start | bytes 589824 | tf_op jit(solution)/shard_map/all_to_all | solution.py:371
  81.1 11.1 %copy-start.4 = (f32[16,3,256]{2,1,0:T(4,128)S(1)}, f32[16,3,256]{2,1,0:T(4,128)}, u32[]{:S(2)}) copy-start(f32[16,3,256]{2,1,0:T(4,128)} %get-tuple-element.16) | copy-start | bytes 147460
  81.1 22.3 %all-to-all-start.2 = ((f32[32,2,9,128]{3,1,2,0:T(2,128)}), f32[32,2,9,128]{3,1,2,0:T(2,128)S(1)}, u32[]{:S(2)}, u32[]{:S(2)}) async-start(f32[32,2,9,128]{3,1,2,0:T(2,128)} %copy.40), calls=%async_computation.2 | async-start | bytes 589824 | tf_op jit(solution)/shard_map/all_to_all | solution.py:371
  104.3 1.2 %copy-start.1 = (f32[32,55,128]{2,0,1:T(8,128)S(1)}, f32[32,55,128]{2,0,1:T(8,128)}, u32[]{:S(2)}) copy-start(f32[32,55,128]{2,0,1:T(8,128)} %param.11) | copy-start | bytes 2703364
  104.3 1.4 %copy-start.2 = (f32[32,55,128]{2,0,1:T(8,128)S(1)}, f32[32,55,128]{2,0,1:T(8,128)}, u32[]{:S(2)}) copy-start(f32[32,55,128]{2,0,1:T(8,128)} %param.10) | copy-start | bytes 2703364
